TPU v7x, 8 devices: a whole 2x2x1 slice. The times are simulated.
8 devices in a mesh: dp: 1 (over z), sp: 8 (over y, x, core).
Axes of the slice: x: 2, y: 2, z: 1, core: 2. Of those that a mesh axis runs over, the one named last changes fastest.
Arguments:
- x: bfloat16 [8, 4096], P('dp')
- lens: int32 [8], P('dp')
- wq: bfloat16 [2, 4096, 4096], replicated
- wk: bfloat16 [2, 4096, 1024], replicated
- wv: bfloat16 [2, 4096, 1024], replicated
- wo: bfloat16 [2, 4096, 4096], P(None, 'sp')
- w1: bfloat16 [2, 4096, 16384], P(None, None, 'sp')
- w2: bfloat16 [2, 16384, 4096], P(None, 'sp')
- g1: bfloat16 [2, 4096], replicated
- g2: bfloat16 [2, 4096], replicated
- kc: bfloat16 [2, 8, 4096, 8, 128], P(None, 'dp', 'sp')
- vc: bfloat16 [2, 8, 4096, 8, 128], P(None, 'dp', 'sp')
Outputs:
- output 1: bfloat16 [8, 4096], P('dp')
- output 2: bfloat16 [2, 8, 4096, 8, 128], P(None, 'dp', 'sp')
- output 3: bfloat16 [2, 8, 4096, 8, 128], P(None, 'dp', 'sp')
All inputs are finite; a program needn't handle non-finite values.
Results may differ from a plain program's by a relative error of at most 0.00860115.
Values are sent between devices in bfloat16 or wider.
A program may use at most 1 GiB of HBM per device.

v0:
```python
import jax
import jax.numpy as jnp
from jax import lax
from jax.sharding import PartitionSpec as P

EPS = 1e-6


def _rms(h, g):
    r = lax.rsqrt(jnp.mean(h * h, axis=-1, keepdims=True) + EPS)
    return (h * r * g.astype(jnp.float32)).astype(jnp.bfloat16)


def _mm(a, w):
    return jnp.dot(a, w, preferred_element_type=jnp.float32)


def solution(mesh):
    sp = mesh.shape['sp']
    kspec = P(None, 'dp', 'sp', None, None)

    def local(x, lens, wq, wk, wv, wo, w1, w2, g1, g2, kc, vc):
        nl, b, s_dev, kvh, dh = kc.shape
        hq = wq.shape[-1] // dh
        grp = hq // kvh
        hl = hq // sp
        idx = lax.axis_index('sp')
        posn = idx * s_dev + jnp.arange(s_dev)
        write = (posn[None, :] == (lens - 1)[:, None])[:, :, None, None]
        valid = (posn[None, :] < lens[:, None])[:, None, None, :]
        h = x.astype(jnp.float32)
        ks, vs = [], []
        for l in range(nl):
            xn = _rms(h, g1[l])
            q = _mm(xn, wq[l]).astype(jnp.bfloat16).reshape(b, kvh, grp, dh)
            k = _mm(xn, wk[l]).astype(jnp.bfloat16).reshape(b, 1, kvh, dh)
            v = _mm(xn, wv[l]).astype(jnp.bfloat16).reshape(b, 1, kvh, dh)
            kl = jnp.where(write, k, kc[l])
            vl = jnp.where(write, v, vc[l])
            ks.append(kl)
            vs.append(vl)
            s = jnp.einsum('bkgd,bskd->bkgs', q, kl, preferred_element_type=jnp.float32) * dh ** -0.5
            s = jnp.where(valid, s, -jnp.inf)
            m = jnp.max(s, axis=-1)
            p = jnp.exp(s - jnp.where(jnp.isfinite(m), m, 0.0)[..., None])
            den = jnp.sum(p, axis=-1)
            o = jnp.einsum('bkgs,bskd->bkgd', p.astype(jnp.bfloat16), vl, preferred_element_type=jnp.float32)
            c = jnp.exp(m - lax.pmax(m, 'sp'))
            o, den = lax.psum((o * c[..., None], den * c), 'sp')
            att = (o / den[..., None]).astype(jnp.bfloat16).reshape(b, hq, dh)
            att = lax.dynamic_slice_in_dim(att, idx * hl, hl, axis=1).reshape(b, hl * dh)
            h = h + lax.psum(_mm(att, wo[l]), 'sp')
            u = jax.nn.gelu(_mm(_rms(h, g2[l]), w1[l])).astype(jnp.bfloat16)
            h = h + lax.psum(_mm(u, w2[l]), 'sp')
        return h.astype(jnp.bfloat16), jnp.stack(ks), jnp.stack(vs)

    return jax.shard_map(
        local, mesh=mesh,
        in_specs=(P('dp', None), P('dp'), P(), P(), P(), P(None, 'sp', None), P(None, None, 'sp'),
                  P(None, 'sp', None), P(), P(), kspec, kspec),
        out_specs=(P('dp', None), kspec, kspec), check_vma=False)
```

profile of v0, /device:TPU:0, one launch (start us, length us, event | category | flops | bytes accessed | tf_op | source)
XLA Modules:
  0.0 453.1 jit_solution(10447084968630456606)
XLA Ops:
  9.7 4.6 %fusion.89 = bf16[8,8,128]{2,0,1:T(8,128)(2,1)S(1)} fusion(bf16[2,4096,1024]{2,1,0:T(8,128)(2,1)} %param.15, bf16[8,4096]{1,0:T(8,128)(2,1)} %param.12, f32[4096]{0:T(1024)S(1)} %bitcast.105, f32[8]{0:T(128)S(1)} %add_rsqrt_fusion.3), kind=kOutput, calls=%fused_computation.69 | convolution fusion | flops 67248128 | bytes 8486944 | tf_op jit(solution)/shard_map/dot_general | solution.py:15
  14.4 4.6 %fusion.86 = bf16[8,8,128]{2,0,1:T(8,128)(2,1)S(1)} fusion(bf16[2,4096,1024]{2,1,0:T(8,128)(2,1)} %param.16, bf16[8,4096]{1,0:T(8,128)(2,1)S(1)} %copy-done, f32[4096]{0:T(1024)S(1)} %bitcast.106, f32[8]{0:T(128)S(1)} %add_rsqrt_fusion.3), kind=kOutput, calls=%fused_computation.68 | convolution fusion | flops 67248128 | bytes 8486944 | tf_op jit(solution)/shard_map/dot_general | solution.py:15
  19.0 12.9 %fusion.38 = bf16[8,4096]{1,0:T(8,128)(2,1)S(1)} fusion(bf16[2,4096,4096]{2,1,0:T(8,128)(2,1)} %param.14, bf16[8,4096]{1,0:T(8,128)(2,1)S(1)} %copy-done, f32[4096]{0:T(1024)S(1)} %bitcast.107, f32[8]{0:T(128)S(1)} %add_rsqrt_fusion.3), kind=kOutput, calls=%fused_computation.48 | convolution fusion | flops 268599296 | bytes 33701920 | tf_op jit(solution)/shard_map/dot_general | solution.py:15
  32.0 15.6 %bitcast_select_fusion.3 = (bf16[8,512,8,128]{3,2,1,0:T(8,128)(2,1)S(1)}, bf16[8,512,8,128]{3,2,1,0:T(8,128)(2,1)}) fusion(pred[8,512]{1,0:T(8,128)(4,1)S(1)} %get-tuple-element.26, bf16[2,8,512,8,128]{4,3,2,1,0:T(8,128)(2,1)} %param.22, bf16[8,8,128]{2,1,0:T(8,128)(2,1)S(1)} %copy.15, bf16[2,8,512,8,128]{4,3,2,1,0:T(8,128)(2,1)} %param.23, ...), kind=kLoop, calls=%fused_computation.29 | loop fusion | flops 8388608 | bytes 33591296 | tf_op jit(solution)/shard_map/jit(_where)/select_n | solution.py:38
  47.5 2.4 fusion.168
  50.0 25.2 %pmax.14 = f32[8,8,4]{2,1,0:T(8,128)S(1)} all-reduce(f32[8,8,4]{2,1,0:T(8,128)S(1)} %get-tuple-element.27), channel_id=1, replica_groups=mesh['dp'=1,'sp'=8] {'sp'}, use_global_device_ids=true, to_apply=%region_2.3 | all-reduce | flops 256 | bytes 2048 | tf_op jit(solution)/shard_map/pmax | solution.py:48
  75.6 5.6 %fusion.56 = f32[8,8,4,128]{3,2,1,0:T(4,128)} fusion(bf16[8,512,8,128]{3,2,1,0:T(8,128)(2,1)} %get-tuple-element.24, f32[8,8,4,512]{3,2,1,0:T(4,128)S(1)} %get-tuple-element.28, f32[8,8,4]{2,1,0:T(8,128)S(1)} %is-finite_select_fusion.1, f32[8,8,4]{2,1,0:T(8,128)S(1)} %get-tuple-element.10), kind=kOutput, calls=%fused_computation.58 | convolution fusion | flops 33849344 | bytes 9046016 | tf_op jit(solution)/shard_map/bkgs,bskd->bkgd/dot_general | solution.py:47
  81.3 23.2 %psum.57 = f32[8,8,4]{2,1,0:T(8,128)S(1)} all-reduce(f32[8,8,4]{2,1,0:T(8,128)S(1)} %get-tuple-element.9), channel_id=1, replica_groups=mesh['dp'=1,'sp'=8] {'sp'}, use_global_device_ids=true, to_apply=%region_5.6 | all-reduce | flops 256 | bytes 2048 | tf_op jit(solution)/shard_map/psum | solution.py:49
  104.5 19.8 %all-reduce.7.cloned.1.call-done = f32[8,8,4,128]{3,2,1,0:T(4,128)} async-done(((f32[8,8,4,128]{3,2,1,0:T(4,128)}), f32[8,8,4,128]{3,2,1,0:T(4,128)}) %all-reduce.7.cloned.1.call-update) | async-done | bytes 131088 | tf_op jit(solution)/shard_map/psum | solution.py:49
  125.4 3.5 fusion.46
  129.2 41.4 %all-reduce.9.cloned.1.call-done = f32[8,4096]{1,0:T(8,128)} async-done(((f32[8,4096]{1,0:T(8,128)}), f32[8,4096]{1,0:T(8,128)}) %all-reduce.9.cloned.1.call-update) | async-done | bytes 131088 | tf_op jit(solution)/shard_map/psum | solution.py:52
  170.6 1.1 multiply_reduce_fusion.2
  171.7 15.6 %fusion.10 = f32[8,4096]{1,0:T(8,128)} fusion(bf16[2,2048,4096]{2,1,0:T(8,128)(2,1)} %param.19, bf16[2,4096,2048]{2,1,0:T(8,128)(2,1)} %param.18, f32[4096]{0:T(1024)S(1)} %bitcast.113, f32[8]{0:T(128)S(1)} %add_rsqrt_fusion.2, f32[8,4096]{1,0:T(8,128)} %all-reduce.9.cloned.1.call-done, bf16[8,4096]{1,0:T(8,128)(2,1)S(1)} %copy-done), kind=kOutput, calls=%fused_computation.12 | convolution fusion | flops 268746752 | bytes 33898528 | tf_op jit(solution)/shard_map/dot_general | solution.py:15
  187.3 41.6 %all-reduce.11.cloned.1.call-done = f32[8,4096]{1,0:T(8,128)} async-done(((f32[8,4096]{1,0:T(8,128)}), f32[8,4096]{1,0:T(8,128)}) %all-reduce.11.cloned.1.call-update) | async-done | bytes 131088 | tf_op jit(solution)/shard_map/psum | solution.py:54
  229.0 1.1 multiply_reduce_fusion.1
  230.1 4.6 %fusion.80 = bf16[8,8,128]{2,0,1:T(8,128)(2,1)S(1)} fusion(bf16[8,4096]{1,0:T(8,128)(2,1)S(1)} %multiply_convert_fusion.1, bf16[2,4096,1024]{2,1,0:T(8,128)(2,1)} %param.16), kind=kOutput, calls=%fused_computation.66 | convolution fusion | flops 67117056 | bytes 8470528 | tf_op jit(solution)/shard_map/dot_general | solution.py:15
  234.7 4.6 %fusion.83 = bf16[8,8,128]{2,0,1:T(8,128)(2,1)S(1)} fusion(bf16[8,4096]{1,0:T(8,128)(2,1)S(1)} %multiply_convert_fusion.1, bf16[2,4096,1024]{2,1,0:T(8,128)(2,1)} %param.15), kind=kOutput, calls=%fused_computation.67 | convolution fusion | flops 67117056 | bytes 8470528 | tf_op jit(solution)/shard_map/dot_general | solution.py:15
  239.3 12.8 %fusion.41 = bf16[8,4096]{1,0:T(8,128)(2,1)S(1)} fusion(bf16[8,4096]{1,0:T(8,128)(2,1)S(1)} %multiply_convert_fusion.1, bf16[2,4096,4096]{2,1,0:T(8,128)(2,1)} %param.14), kind=kOutput, calls=%fused_computation.49 | convolution fusion | flops 268468224 | bytes 33685504 | tf_op jit(solution)/shard_map/dot_general | solution.py:15
  252.1 15.6 %bitcast_select_fusion.1 = (bf16[8,512,8,128]{3,2,1,0:T(8,128)(2,1)S(1)}, bf16[8,512,8,128]{3,2,1,0:T(8,128)(2,1)}) fusion(pred[8,512]{1,0:T(8,128)(4,1)S(1)} %get-tuple-element.26, bf16[2,8,512,8,128]{4,3,2,1,0:T(8,128)(2,1)} %param.22, bf16[8,8,128]{2,1,0:T(8,128)(2,1)S(1)} %copy.20, bf16[2,8,512,8,128]{4,3,2,1,0:T(8,128)(2,1)} %param.23, ...), kind=kLoop, calls=%fused_computation.23 | loop fusion | flops 8388608 | bytes 33591296 | tf_op jit(solution)/shard_map/jit(_where)/select_n | solution.py:38
  267.7 2.4 fusion.169
  270.2 22.6 %pmax.15 = f32[8,8,4]{2,1,0:T(8,128)S(1)} all-reduce(f32[8,8,4]{2,1,0:T(8,128)S(1)} %get-tuple-element.29), channel_id=1, replica_groups=mesh['dp'=1,'sp'=8] {'sp'}, use_global_device_ids=true, to_apply=%region_11.12 | all-reduce | flops 256 | bytes 2048 | tf_op jit(solution)/shard_map/pmax | solution.py:48
  293.2 5.6 %fusion.59 = f32[8,8,4,128]{3,2,1,0:T(4,128)} fusion(bf16[8,512,8,128]{3,2,1,0:T(8,128)(2,1)} %get-tuple-element.22, f32[8,8,4,512]{3,2,1,0:T(4,128)S(1)} %get-tuple-element.30, f32[8,8,4]{2,1,0:T(8,128)S(1)} %is-finite_select_fusion, f32[8,8,4]{2,1,0:T(8,128)S(1)} %get-tuple-element.6), kind=kOutput, calls=%fused_computation.59 | convolution fusion | flops 33849344 | bytes 9046016 | tf_op jit(solution)/shard_map/bkgs,bskd->bkgd/dot_general | solution.py:47
  298.8 23.5 %psum.61 = f32[8,8,4]{2,1,0:T(8,128)S(1)} all-reduce(f32[8,8,4]{2,1,0:T(8,128)S(1)} %get-tuple-element.5), channel_id=1, replica_groups=mesh['dp'=1,'sp'=8] {'sp'}, use_global_device_ids=true, to_apply=%region_14.15 | all-reduce | flops 256 | bytes 2048 | tf_op jit(solution)/shard_map/psum | solution.py:49
  322.4 19.8 %all-reduce.13.cloned.1.call-done = f32[8,8,4,128]{3,2,1,0:T(4,128)} async-done(((f32[8,8,4,128]{3,2,1,0:T(4,128)}), f32[8,8,4,128]{3,2,1,0:T(4,128)}) %all-reduce.13.cloned.1.call-update) | async-done | bytes 131088 | tf_op jit(solution)/shard_map/psum | solution.py:49
  343.2 3.5 fusion.44
  346.8 22.9 %broadcast_select_fusion.1 = (bf16[1,8,512,8,128]{4,3,2,1,0:T(8,128)(2,1)}, bf16[1,8,512,8,128]{4,3,2,1,0:T(8,128)(2,1)}, bf16[1,8,512,8,128]{4,3,2,1,0:T(8,128)(2,1)}, bf16[1,8,512,8,128]{4,3,2,1,0:T(8,128)(2,1)}) fusion(pred[8,512]{1,0:T(8,128)(4,1)S(1)} %get-tuple-element.26, bf16[2,8,512,8,128]{4,3,2,1,0:T(8,128)(2,1)} %param.23, ...), kind=kLoop, calls=%fused_computation.45 | loop fusion | flops 16777216 | bytes 67178496 | tf_op jit(solution)/shard_map/jit(_where)/select_n | solution.py:39
  369.7 18.7 %all-reduce.15.cloned.1.call-done = f32[8,4096]{1,0:T(8,128)} async-done(((f32[8,4096]{1,0:T(8,128)}), f32[8,4096]{1,0:T(8,128)}) %all-reduce.15.cloned.1.call-update) | async-done | bytes 131088 | tf_op jit(solution)/shard_map/psum | solution.py:52
  388.4 1.1 multiply_reduce_fusion
  389.5 13.5 %fusion.6 = f32[8,4096]{1,0:T(8,128)} fusion(bf16[2,2048,4096]{2,1,0:T(8,128)(2,1)} %param.19, bf16[2,4096,2048]{2,1,0:T(8,128)(2,1)} %param.18, f32[8,4096]{1,0:T(8,128)S(1)} %get-tuple-element.4, f32[4096]{0:T(1024)S(1)} %bitcast.112, f32[8]{0:T(128)S(1)} %add_rsqrt_fusion), kind=kOutput, calls=%fused_computation.8 | convolution fusion | flops 268681216 | bytes 33832992 | tf_op jit(solution)/shard_map/dot_general | solution.py:15
  403.0 22.8 %pad_maximum_fusion = (bf16[2,8,512,8,128]{4,3,2,1,0:T(8,128)(2,1)}, bf16[2,8,512,8,128]{4,3,2,1,0:T(8,128)(2,1)}) fusion(bf16[1,8,512,8,128]{4,3,2,1,0:T(8,128)(2,1)} %get-tuple-element.19, bf16[1,8,512,8,128]{4,3,2,1,0:T(8,128)(2,1)} %get-tuple-element.20, bf16[1,8,512,8,128]{4,3,2,1,0:T(8,128)(2,1)} %get-tuple-element.12, ...), kind=kLoop, calls=%fused_computation.6 | loop fusion | flops 16777216 | bytes 67108864 | tf_op jit(solution)/shard_map/stack | solution.py:55
  425.8 18.9 %all-reduce.17.cloned.1.call-done = f32[8,4096]{1,0:T(8,128)} async-done(((f32[8,4096]{1,0:T(8,128)}), f32[8,4096]{1,0:T(8,128)}) %all-reduce.17.cloned.1.call-update) | async-done | bytes 131088 | tf_op jit(solution)/shard_map/psum | solution.py:54
  444.7 1.5 add_convert_fusion
  (45 shorter events, 6.1 us)
Async XLA Ops:
  7.2 7.2 %copy-start = (bf16[8,4096]{1,0:T(8,128)(2,1)S(1)}, bf16[8,4096]{1,0:T(8,128)(2,1)}, u32[]{:S(2)}) copy-start(bf16[8,4096]{1,0:T(8,128)(2,1)} %param.12) | copy-start | bytes 196612
  7.2 117.1 %all-reduce.7.cloned.1.call-start = ((), (), s32[]{:S(2)}) async-start(), calls=%async_computation | async-start | bytes 262144 | tf_op jit(solution)/shard_map/psum | solution.py:49
  19.0 12.9 %copy-start.3 = (s32[8]{0:T(128)S(1)}, s32[8]{0:T(128)}, u32[]{:S(2)}) copy-start(s32[8]{0:T(128)} %param.13) | copy-start | bytes 100
  50.0 79.2 %copy-start.2 = (bf16[2,4096]{1,0:T(2,128)(2,1)S(1)}, bf16[2,4096]{1,0:T(2,128)(2,1)}, u32[]{:S(2)}) copy-start(bf16[2,4096]{1,0:T(2,128)(2,1)} %param.21) | copy-start | bytes 49156
  81.2 89.4 %all-reduce.9.cloned.1.call-start = ((), (), s32[]{:S(2)}) async-start(), calls=%async_computation.1 | async-start | bytes 262144 | tf_op jit(solution)/shard_map/psum | solution.py:52
  128.9 100.0 %all-reduce.11.cloned.1.call-start = ((), (), s32[]{:S(2)}) async-start(), calls=%async_computation.2 | async-start | bytes 262144 | tf_op jit(solution)/shard_map/psum | solution.py:54
  171.6 57.3 %copy-start.1 = (f32[8,4096]{1,0:T(8,128)S(1)}, f32[8,4096]{1,0:T(8,128)}, u32[]{:S(2)}) copy-start(f32[8,4096]{1,0:T(8,128)} %all-reduce.9.cloned.1.call-done) | copy-start | bytes 393220
  187.3 154.8 %all-reduce.13.cloned.1.call-start = ((), (), s32[]{:S(2)}) async-start(), calls=%async_computation.3 | async-start | bytes 262144 | tf_op jit(solution)/shard_map/psum | solution.py:49
  298.8 89.6 %all-reduce.15.cloned.1.call-start = ((), (), s32[]{:S(2)}) async-start(), calls=%async_computation.4 | async-start | bytes 262144 | tf_op jit(solution)/shard_map/psum | solution.py:52
  346.7 98.0 %all-reduce.17.cloned.1.call-start = ((), (), s32[]{:S(2)}) async-start(), calls=%async_computation.5 | async-start | bytes 262144 | tf_op jit(solution)/shard_map/psum | solution.py:54
Sparse Core Ops, SparseCore 0:
  81.3 42.9 all-reduce.6
  129.0 41.5 all-reduce.8
  187.4 41.5 all-reduce.10
  298.9 43.1 all-reduce.12
  346.9 41.5 all-reduce.14
  403.1 41.5 all-reduce.16
where the time goes:
time: 454 us; the launch traced here: 453 us
  waiting for transfers between devices  160 us (35%)
  matrix products  96.3 us (21%)
  blocking collectives  94.6 us (21%)
  other arithmetic  87.1 us (19%)
  between operations  14.3 us (3%)
    dot_general x10, matrix products, _mm(): return jnp.dot(a, w, preferred_element_type=jnp.float32)  80.3 us
    psum x2, waiting for transfers between devices, local(): h = h + lax.psum(_mm(u, w2[l]), 'sp')  60.5 us
    psum x2, waiting for transfers between devices, local(): h = h + lax.psum(_mm(att, wo[l]), 'sp')  60.1 us
    pmax x2, blocking collectives, local(): c = jnp.exp(m - lax.pmax(m, 'sp'))  47.9 us
    psum x2, blocking collectives, local(): o, den = lax.psum((o * c[..., None], den * c), 'sp')  46.7 us
    psum x2, waiting for transfers between devices, local(): o, den = lax.psum((o * c[..., None], den * c), 'sp')  39.6 us
    select_n x2, other arithmetic, local(): kl = jnp.where(write, k, kc[l])  31.2 us
    select_n x1, other arithmetic, local(): vl = jnp.where(write, v, vc[l])  22.9 us
  transfers between devices with their start and end apart: 6, of which 6 were waited for; matrix products, arithmetic and copies ran while one was open for 10% of the time, Pallas kernels for 0%

commit v1 on v0

v1 whole, which is shorter than its diff:
```python
import functools

import jax
import jax.numpy as jnp
from jax import lax
from jax.experimental import pallas as pl
from jax.experimental.pallas import tpu as pltpu
from jax.sharding import PartitionSpec as P

EPS = 1e-6
N = 8
B = 8
D = 4096
KVH = 8
G = 4
DH = 128
SD = 512
R = SD * KVH
C = D // N
QW = (G + 2) * DH
FD = 2048
FC = 512
NF = FD // FC
SCALE = DH ** -0.5
F32, BF16 = jnp.float32, jnp.bfloat16
MESH = pl.DeviceIdType.MESH
VM = pl.BlockSpec(memory_space=pltpu.VMEM)
HBM = pl.BlockSpec(memory_space=pltpu.HBM)
SM = pl.BlockSpec(memory_space=pltpu.SMEM)
LIMIT = 67_043_328
DMA = pltpu.SemaphoreType.DMA
SDS = jax.ShapeDtypeStruct


def _peer(me, m):
    return ((me // 4 + m // 4) % 2) * 4 + ((me // 2 + m // 2) % 2) * 2 + (me + m) % 2


def _remote(src, dst, ssem, rsem, dev):
    return pltpu.make_async_remote_copy(src_ref=src, dst_ref=dst, send_sem=ssem, recv_sem=rsem,
                                        device_id={'sp': dev}, device_id_type=MESH)


def _barrier(me):
    bar = pltpu.get_barrier_semaphore()
    for m in range(1, N):
        pl.semaphore_signal(bar, inc=1, device_id={'sp': _peer(me, m)}, device_id_type=MESH)
    pl.semaphore_wait(bar, N - 1)


def _dot(a, w):
    return jnp.dot(a, w, preferred_element_type=F32)


def _qkv_copies(l, me, wq, wk, wv, wqb, wkvb, sem):
    cols = pl.ds(pl.multiple_of(me * G * DH, G * DH), G * DH)
    one = pl.ds(pl.multiple_of(me * DH, DH), DH)
    return (pltpu.make_async_copy(wq.at[l, :, cols], wqb, sem.at[0]),
            pltpu.make_async_copy(wk.at[l, :, one], wkvb.at[0], sem.at[1]),
            pltpu.make_async_copy(wv.at[l, :, one], wkvb.at[1], sem.at[2]))


def _qkv(xn, wqb, wkvb, cps, out):
    cps[0].wait()
    out[:, :G * DH] = _dot(xn, wqb[...]).astype(BF16)
    cps[1].wait()
    cps[2].wait()
    out[:, G * DH:(G + 1) * DH] = _dot(xn, wkvb[0]).astype(BF16)
    out[:, (G + 1) * DH:] = _dot(xn, wkvb[1]).astype(BF16)


def _bcast_start(me, buf, ssem, rsem):
    def body(t, _):
        _remote(buf.at[me], buf.at[me], ssem.at[t], rsem.at[me], _peer(me, 7 - t)).start()
        return 0
    lax.fori_loop(0, N - 1, body, 0)


def _bcast_wait(me, buf, ssem, rsem):
    def body(t, _):
        s = _peer(me, 1 + t)
        _remote(buf.at[me], buf.at[s], ssem.at[t], rsem.at[s], s).wait_recv()
        return 0
    lax.fori_loop(0, N - 1, body, 0)

    def done(t, _):
        _remote(buf.at[me], buf.at[me], ssem.at[t], rsem.at[me], _peer(me, 7 - t)).wait_send()
        return 0
    lax.fori_loop(0, N - 1, done, 0)


def _split_heads(qkv, qf):
    for j in range(G + 2):
        qf[j] = qkv[:, :, j * DH:(j + 1) * DH].astype(F32).reshape(N * B, DH)


def _attend(b, lim, qf, kb, vb, o_out, ml_out):
    q = jnp.concatenate([qf[g, pl.ds(b, KVH, stride=B), :] for g in range(G)], axis=0).astype(BF16)
    s = lax.dot_general(q, kb, (((1,), (1,)), ((), ())), preferred_element_type=F32) * SCALE
    col = lax.broadcasted_iota(jnp.int32, s.shape, 1)
    row = lax.broadcasted_iota(jnp.int32, s.shape, 0)
    s = jnp.where(((col & 7) == (row & 7)) & (col < lim * KVH), s, -jnp.inf)
    m = jnp.max(s, axis=-1, keepdims=True)
    p = jnp.exp(s - jnp.where(m == -jnp.inf, 0.0, m))
    den = jnp.sum(p, axis=-1, keepdims=True)
    o = _dot(p.astype(BF16), vb)
    lane = lax.broadcasted_iota(jnp.int32, (KVH, DH), 1)
    ml = jnp.zeros((KVH, DH), F32)
    for g in range(G):
        rows = slice(g * KVH, (g + 1) * KVH)
        o_out[pl.ds(g * B + b, KVH, stride=G * B), :] = o[rows]
        ml = jnp.where(lane == g, m[rows], ml)
        ml = jnp.where(lane == G + g, den[rows], ml)
    ml_out[pl.ds(b, KVH, stride=B), :] = ml


def _new_rows(b, qf, k_out, v_out):
    k_out[b] = qf[G, pl.ds(b, KVH, stride=B), :].astype(BF16)
    v_out[b] = qf[G + 1, pl.ds(b, KVH, stride=B), :].astype(BF16)


def _k1(x, g1, wq, wk, wv, qkv, xn, wqb, wkvb, wsem, ssem, rsem):
    me = lax.axis_index('sp')
    cps = _qkv_copies(0, me, wq, wk, wv, wqb, wkvb, wsem)
    for c in cps:
        c.start()
    h = x[...].astype(F32)
    r = lax.rsqrt(jnp.mean(h * h, axis=-1, keepdims=True) + EPS)
    xn[...] = (h * r * g1[0:1, :].astype(F32)).astype(BF16)
    _barrier(me)
    _qkv(xn[...], wqb, wkvb, cps, qkv.at[me])
    _bcast_start(me, qkv, ssem, rsem)
    _bcast_wait(me, qkv, ssem, rsem)


def _k2(lens, qkv, kc, vc, kn, vn, o, ml, k0, v0, qf, kb, vb, rsem, wsem):
    me = lax.axis_index('sp')

    def copies(l, b):
        return ((pltpu.make_async_copy(kc.at[l, b], kb.at[l, b], rsem.at[0, l, b]),
                 pltpu.make_async_copy(vc.at[l, b], vb.at[l, b], rsem.at[1, l, b])),
                (pltpu.make_async_copy(kb.at[l, b], kn.at[l, b], wsem.at[0, l, b]),
                 pltpu.make_async_copy(vb.at[l, b], vn.at[l, b], wsem.at[1, l, b])))

    for l in range(2):
        for b in range(B):
            for c in copies(l, b)[0]:
                c.start()
    _split_heads(qkv, qf)

    def turn(l, b):
        rd, wr = copies(l, b)
        for c in rd:
            c.wait()
        for c in wr:
            c.start()

    def body(b, _):
        turn(0, b)
        _new_rows(b, qf, k0, v0)
        _attend(b, lens[b] - 1 - me * SD, qf, kb[0, b], vb[0, b], o, ml)
        return 0
    lax.fori_loop(0, B, body, 0)

    def rest(b, _):
        turn(1, b)
        return 0
    lax.fori_loop(0, B, rest, 0)

    def drain(b, _):
        for l in range(2):
            for c in copies(l, b)[1]:
                c.wait()
        return 0
    lax.fori_loop(0, B, drain, 0)


def _main(x, lens, g1, g2, qkv0, o0, ml0, wq, wk, wv, wo, w1, w2, kc, vc, y, k1, v1,
          wqb, wkvb, wob, w1b, w2b, kb, vb, xn, u, qkv1, qf, o1, orecv, mlrecv, rs_send, rs_recv, ag, yg, ml1,
          qsem, osem, w1sem, w2sem, ksem, vsem, a_s, a_r, m_s, m_r, rs_s, rs_r, ag_s, ag_r, q_s, q_r, y_s, y_r):
    me = lax.axis_index('sp')
    mine = pl.ds(pl.multiple_of(me * C, C), C)

    def wo_copy(l, t):
        cols = pl.ds(pl.multiple_of(_peer(me, 7 - t) * C, C), C)
        return pltpu.make_async_copy(wo.at[l, :, cols], wob.at[t], osem.at[t])

    def w1_copy(l, t):
        return pltpu.make_async_copy(w1.at[l, :, pl.ds(pl.multiple_of(t * FC, FC), FC)], w1b.at[t], w1sem.at[t])

    def w2_copy(l, t):
        cols = pl.ds(pl.multiple_of(_peer(me, 7 - t) * C, C), C)
        return pltpu.make_async_copy(w2.at[l, :, cols], w2b.at[t], w2sem.at[t])

    def kv_copies(b):
        return (pltpu.make_async_copy(kc.at[1, b], kb.at[b], ksem.at[b]),
                pltpu.make_async_copy(vc.at[1, b], vb.at[b], vsem.at[b]))

    for t in range(N):
        wo_copy(0, t).start()
    for t in range(NF):
        w1_copy(0, t).start()
    for t in range(N):
        w2_copy(0, t).start()
    qcps = _qkv_copies(1, me, wq, wk, wv, wqb, wkvb, qsem)
    for c in qcps:
        c.start()
    for b in range(B):
        for c in kv_copies(b):
            c.start()
    _barrier(me)

    def exchange(l, o, ml):
        def cps(t):
            d = _peer(me, 7 - t)
            return (_remote(o.at[pl.ds(pl.multiple_of(d * 32, 32), 32)], orecv.at[l, me], a_s.at[l, t], a_r.at[l, me], d),
                    _remote(ml.at[pl.ds(pl.multiple_of(d * 8, 8), 8)], mlrecv.at[l, me], m_s.at[l, t], m_r.at[l, me], d))

        def start(t, _):
            for c in cps(t):
                c.start()
            return 0
        lax.fori_loop(0, N - 1, start, 0)
        orecv[l, me] = o[pl.ds(pl.multiple_of(me * 32, 32), 32)]
        mlrecv[l, me] = ml[pl.ds(pl.multiple_of(me * 8, 8), 8)]

        def wait(t, _):
            s = _peer(me, 1 + t)
            _remote(o.at[pl.ds(0, 32)], orecv.at[l, s], a_s.at[l, t], a_r.at[l, s], s).wait_recv()
            _remote(ml.at[pl.ds(0, 8)], mlrecv.at[l, s], m_s.at[l, t], m_r.at[l, s], s).wait_recv()
            return 0
        lax.fori_loop(0, N - 1, wait, 0)

        def sent(t, _):
            for c in cps(t):
                c.wait_send()
            return 0
        lax.fori_loop(0, N - 1, sent, 0)

    def combine(l, own):
        k = own[:, G * DH:(G + 1) * DH]
        v = own[:, (G + 1) * DH:]
        out = []
        for g in range(G):
            sn = jnp.sum(own[:, g * DH:(g + 1) * DH] * k, axis=-1, keepdims=True) * SCALE
            ms = [mlrecv[l, s, :, g:g + 1] for s in range(N)]
            mt = functools.reduce(jnp.maximum, ms, sn)
            w = jnp.exp(sn - mt)
            den, num = w, w * v
            for s in range(N):
                w = jnp.exp(ms[s] - mt)
                den = den + w * mlrecv[l, s, :, G + g:G + g + 1]
                num = num + w * orecv[l, s, g * B:(g + 1) * B, :]
            out.append((num / den).astype(BF16))
        return jnp.concatenate(out, axis=-1)

    def reduce_scatter(use, a, wb, wait, again):
        def copy(t):
            return _remote(rs_send.at[use, t], rs_recv.at[use, me], rs_s.at[use, t], rs_r.at[use, me], _peer(me, 7 - t))

        def step(t, _):
            wait(t)
            rs_send[use, t] = _dot(a[...], wb[t])

            @pl.when(t < N - 1)
            def _():
                copy(t).start()
            if again is not None:
                again(t)
            return 0
        lax.fori_loop(0, N, step, 0)

        def add(t, acc):
            s = _peer(me, 1 + t)
            _remote(rs_send.at[use, t], rs_recv.at[use, s], rs_s.at[use, t], rs_r.at[use, s], s).wait_recv()
            return acc + rs_recv[use, s]
        acc = lax.fori_loop(0, N - 1, add, rs_send[use, N - 1])

        def sent(t, _):
            copy(t).wait_send()
            return 0
        lax.fori_loop(0, N - 1, sent, 0)
        return acc

    def gather_norm(use, hs, g):
        ag[use, me] = hs
        _bcast_start(me, ag.at[use], ag_s.at[use], ag_r.at[use])
        _bcast_wait(me, ag.at[use], ag_s.at[use], ag_r.at[use])
        ss = jnp.zeros((B, C), F32)
        for c in range(N):
            ss = ss + ag[use, c] * ag[use, c]
        r = lax.rsqrt(jnp.sum(ss, axis=-1, keepdims=True) / D + EPS)
        for c in range(N):
            xn[:, c * C:(c + 1) * C] = (ag[use, c] * r * g[:, c * C:(c + 1) * C].astype(F32)).astype(BF16)

    def layer(l, own, hs):
        first = l == 0
        u[:, :C] = combine(l, own)
        hs = hs + reduce_scatter(2 * l, u.at[:, :C], wob, lambda t: wo_copy(l, t).wait(),
                                 (lambda t: wo_copy(1, t).start()) if first else None)
        gather_norm(2 * l, hs, g2[l:l + 1, :])

        def up(t, _):
            w1_copy(l, t).wait()
            z = _dot(xn[...], w1b[t])
            u[:, pl.ds(pl.multiple_of(t * FC, FC), FC)] = jax.nn.gelu(z).astype(BF16)
            if first:
                w1_copy(1, t).start()
            return 0
        lax.fori_loop(0, NF, up, 0)
        return hs + reduce_scatter(2 * l + 1, u, w2b, lambda t: w2_copy(l, t).wait(),
                                   (lambda t: w2_copy(1, t).start()) if first else None)

    exchange(0, o0, ml0)
    hs = layer(0, qkv0[me].astype(F32), x[:, mine].astype(F32))
    gather_norm(1, hs, g1[1:2, :])
    _qkv(xn[...], wqb, wkvb, qcps, qkv1.at[me])
    _bcast_start(me, qkv1, q_s, q_r)
    _bcast_wait(me, qkv1, q_s, q_r)
    _split_heads(qkv1, qf)

    def att(b, _):
        for c in kv_copies(b):
            c.wait()
        _new_rows(b, qf, k1, v1)
        _attend(b, lens[b] - 1 - me * SD, qf, kb[b], vb[b], o1, ml1)
        return 0
    lax.fori_loop(0, B, att, 0)
    exchange(1, o1, ml1)
    hs = layer(1, qkv1[me].astype(F32), hs)
    yg[me] = hs.astype(BF16)
    _bcast_start(me, yg, y_s, y_r)
    _bcast_wait(me, yg, y_s, y_r)
    for c in range(N):
        y[:, c * C:(c + 1) * C] = yg[c]


def _k4(lens, y, k0, v0, k1, v1, kin, vin, kn, vn, yo, sem):
    me = lax.axis_index('sp')
    for wait in (False, True):
        for b in range(B):
            p = lens[b] - 1 - me * SD

            @pl.when((p >= 0) & (p < SD))
            def _():
                for i, (src, dst) in enumerate(((k0, kn.at[0]), (v0, vn.at[0]), (k1, kn.at[1]), (v1, vn.at[1]))):
                    c = pltpu.make_async_copy(src.at[b], dst.at[b, jnp.clip(p, 0, SD - 1)], sem.at[i, b])
                    c.wait() if wait else c.start()
        if not wait:
            yo[...] = y[...]


def solution(mesh):
    kspec = P(None, 'dp', 'sp', None, None)

    def local(x, lens, wq, wk, wv, wo, w1, w2, g1, g2, kc, vc):
        kc4, vc4 = (c.reshape(2, B, R, DH) for c in (kc, vc))
        qkv0 = pl.pallas_call(
            _k1, name='k1', out_shape=SDS((N, B, QW), BF16), in_specs=[VM, VM, HBM, HBM, HBM], out_specs=VM,
            scratch_shapes=[pltpu.VMEM((B, D), BF16), pltpu.VMEM((D, G * DH), BF16), pltpu.VMEM((2, D, DH), BF16),
                            DMA((3,)), DMA((N,)), DMA((N,))],
            compiler_params=pltpu.CompilerParams(collective_id=0, has_side_effects=True, vmem_limit_bytes=LIMIT),
        )(x, g1, wq, wk, wv)
        new = SDS((B, KVH, DH), BF16)
        kn, vn, o0, ml0, k0, v0 = pl.pallas_call(
            _k2, name='k2',
            out_shape=(pltpu.HBM(kc4.shape, BF16), pltpu.HBM(vc4.shape, BF16), SDS((N * G * B, DH), F32),
                       SDS((N * B, DH), F32), new, new),
            in_specs=[SM, VM, HBM, HBM], out_specs=(HBM, HBM, VM, VM, VM, VM),
            scratch_shapes=[pltpu.VMEM((G + 2, N * B, DH), F32), pltpu.VMEM((2, B, R, DH), BF16),
                            pltpu.VMEM((2, B, R, DH), BF16), DMA((2, 2, B)), DMA((2, 2, B))],
            compiler_params=pltpu.CompilerParams(vmem_limit_bytes=LIMIT),
        )(lens, qkv0, kc4, vc4)
        y, k1, v1 = pl.pallas_call(
            _main, name='main', out_shape=(SDS((B, D), BF16), new, new),
            in_specs=[VM, SM, VM, VM, VM, VM, VM] + [HBM] * 8, out_specs=(VM, VM, VM),
            scratch_shapes=[
                pltpu.VMEM((D, G * DH), BF16), pltpu.VMEM((2, D, DH), BF16), pltpu.VMEM((N, G * DH, C), BF16),
                pltpu.VMEM((NF, D, FC), BF16), pltpu.VMEM((N, FD, C), BF16), pltpu.VMEM((B, R, DH), BF16),
                pltpu.VMEM((B, R, DH), BF16), pltpu.VMEM((B, D), BF16), pltpu.VMEM((B, FD), BF16),
                pltpu.VMEM((N, B, QW), BF16), pltpu.VMEM((G + 2, N * B, DH), F32), pltpu.VMEM((N * G * B, DH), F32),
                pltpu.VMEM((2, N, G * B, DH), F32), pltpu.VMEM((2, N, B, DH), F32), pltpu.VMEM((4, N, B, C), F32),
                pltpu.VMEM((4, N, B, C), F32), pltpu.VMEM((3, N, B, C), F32), pltpu.VMEM((N, B, C), BF16),
                pltpu.VMEM((N * B, DH), F32),
                DMA((3,)), DMA((N,)), DMA((NF,)), DMA((N,)), DMA((B,)), DMA((B,)),
                DMA((2, N)), DMA((2, N)), DMA((2, N)), DMA((2, N)), DMA((4, N)), DMA((4, N)), DMA((3, N)), DMA((3, N)),
                DMA((N,)), DMA((N,)), DMA((N,)), DMA((N,))],
            compiler_params=pltpu.CompilerParams(collective_id=1, has_side_effects=True, vmem_limit_bytes=LIMIT),
        )(x, lens, g1, g2, qkv0, o0, ml0, wq, wk, wv, wo, w1, w2, kc4, vc4)
        shape = kc.shape
        kn, vn, y = pl.pallas_call(
            _k4, name='k4', out_shape=(pltpu.HBM(shape, BF16), pltpu.HBM(shape, BF16), SDS((B, D), BF16)),
            in_specs=[SM, VM, VM, VM, VM, VM, HBM, HBM], out_specs=(HBM, HBM, VM), input_output_aliases={6: 0, 7: 1},
            scratch_shapes=[DMA((4, B))],
            compiler_params=pltpu.CompilerParams(vmem_limit_bytes=LIMIT),
        )(lens, y, k0, v0, k1, v1, kn.reshape(shape), vn.reshape(shape))
        return y, kn, vn

    return jax.shard_map(
        local, mesh=mesh,
        in_specs=(P('dp', None), P('dp'), P(), P(), P(), P(None, 'sp', None), P(None, None, 'sp'),
                  P(None, 'sp', None), P(), P(), kspec, kspec),
        out_specs=(P('dp', None), kspec, kspec), check_vma=False)
```

time: 454 us -> 107 us (0.24)
  waiting for transfers between devices: 160 us -> 0 us
  Pallas kernels: 0 us -> 106 us
  matrix products: 96.3 us -> 0 us
  blocking collectives: 94.6 us -> 0 us
  other arithmetic: 87.1 us -> 0 us
  between operations: 14.3 us -> 0.65 us
    psum x6 -> x0, waiting for transfers between devices: 160 us -> none  [the longest x2 60.5 us: local(): h = h + lax.psum(_mm(u, w2[l]), 'sp')]
    pallas_call x0 -> x4, Pallas kernels: none -> 106 us  [the longest x1 68.4 us: local(): pl.pallas_call(_main, name='main', out_shape=(SDS((B, D), BF16), new, new...]
    dot_general x14 -> x0, matrix products: 96.3 us -> none  [the longest x10 80.3 us: _mm(): return jnp.dot(a, w, preferred_element_type=jnp.float32)]
    select_n x5 -> x0, other arithmetic: 54.1 us -> none  [the longest x2 31.2 us: local(): kl = jnp.where(write, k, kc[l])]
    pmax x2 -> x0, blocking collectives: 47.9 us -> none  [local(): c = jnp.exp(m - lax.pmax(m, 'sp'))]
    psum x2 -> x0, blocking collectives: 46.7 us -> none  [local(): o, den = lax.psum((o * c[..., None], den * c), 'sp')]
    another operation x1 -> x0, other arithmetic: 22.8 us -> none  [local(): return (h.astype(jnp.bfloat16), jnp.stack(ks), jnp.stack(vs))]
    reduce_sum x6 -> x0, other arithmetic: 4.85 us -> none  [the longest x4 4.14 us: _rms(): r = lax.rsqrt(jnp.mean(h * h, axis=-1, keepdims=True) + EPS)]
  transfers between devices with their start and end apart: 6 -> 0, of which waited for: 6 -> 0; matrix products, arithmetic and copies ran while one was open for 10% -> 0% of each run, Pallas kernels for 0% -> 0%
where the time goes in v1:
time: 107 us
  Pallas kernels  106 us (99%)
    pallas_call x1, Pallas kernels, local(): pl.pallas_call(_main, name='main', out_shape=(SDS((B, D), BF16), new, new...  68.4 us
    pallas_call x1, Pallas kernels, local(): pl.pallas_call(_k2, name='k2', out_shape=(pltpu.HBM(kc4.shape, BF16), plt...  24.4 us
    pallas_call x1, Pallas kernels, local(): pl.pallas_call(_k1, name='k1', out_shape=SDS((N, B, QW), BF16), in_specs=...  11 us
    pallas_call x1, Pallas kernels, local(): pl.pallas_call(_k4, name='k4', out_shape=(pltpu.HBM(shape, BF16), pltpu.H...  2.47 us

profile of v1, /device:TPU:0, one launch (start us, length us, event | category | flops | bytes accessed | tf_op | source)
XLA Modules:
  0.0 107.0 jit_solution(1094817301246465092)
XLA Ops:
  0.6 11.0 %k1.1.qkv.qkv0 = bf16[8,8,768]{2,1,0:T(8,128)(2,1)} custom-call(bf16[8,4096]{1,0:T(8,128)(2,1)} %x.3, bf16[2,4096]{1,0:T(2,128)(2,1)} %g1.3, bf16[2,4096,4096]{2,1,0:T(8,128)(2,1)} %wq.3, bf16[2,4096,1024]{2,1,0:T(8,128)(2,1)} %wk.3, bf16[2,4096,1024]{2,1,0:T(8,128)(2,1)} %wv.3), custom_call_target="tpu_custom_call" | custom-call | tf_op jit(solution)/shard_map/k1/pallas_call | solution.py:358
  11.7 24.4 %k2.1 = (bf16[2,8,4096,128]{3,2,1,0:T(8,128)(2,1)}, bf16[2,8,4096,128]{3,2,1,0:T(8,128)(2,1)}, f32[256,128]{1,0:T(8,128)}, f32[64,128]{1,0:T(8,128)}, bf16[8,8,1...) custom-call(s32[8]{0:T(128)} %lens.5, bf16[8,8,768]{2,1,0:T(8,128)(2,1)} %k1.1.qkv.qkv0, bf16[2,8,4096,128]{3,2,1,0:T(8,128)(2,1)} %bitcast.4, ...), custom_call_target="tpu_custom_call" | custom-call | tf_op jit(solution)/shard_map/k2/pallas_call | solution.py:365
  36.1 68.4 %main.1 = (bf16[8,4096]{1,0:T(8,128)(2,1)}, bf16[8,8,128]{2,1,0:T(8,128)(2,1)}, bf16[8,8,128]{2,1,0:T(8,128)(2,1)}) custom-call(bf16[8,4096]{1,0:T(8,128)(2,1)} %x.3, s32[8]{0:T(128)} %lens.5, bf16[2,4096]{1,0:T(2,128)(2,1)} %g1.3, bf16[2,4096]{1,0:T(2,128)(2,1)} %g2.1, bf16[8,8,768]{2,1,0:T(8,128)(2,1)} %k1.1.qkv.qkv0, f32[256,128]{1,0:T(8,128)} %get-tuple-element.15.o0, ...), custom_call_target="tpu_custom_call" | custom-call | tf_op jit(solution)/shard_map/main/pallas_call | solution.py:374
  104.5 2.5 %k4.1 = (bf16[2,8,512,8,128]{4,3,2,1,0:T(8,128)(2,1)}, bf16[2,8,512,8,128]{4,3,2,1,0:T(8,128)(2,1)}, bf16[8,4096]{1,0:T(8,128)(2,1)}) custom-call(s32[8]{0:T(128)} %lens.5, bf16[8,4096]{1,0:T(8,128)(2,1)} %get-tuple-element.17.y, bf16[8,8,128]{2,1,0:T(8,128)(2,1)} %get-tuple-element.18.k0, ...), custom_call_target="tpu_custom_call", output_to_operand_aliasing={{0}: (6, {}), {1}: (7, {})} | custom-call | tf_op jit(solution)/shard_map/k4/pallas_call | solution.py:391
